TPU v7x, 32 devices: a whole 2x2x4 slice. The times are simulated.
32 devices in a mesh: parts: 2 (over x), shard: 16 (over z, y, core).
Axes of the slice: x: 2, y: 2, z: 4, core: 2. Of those that a mesh axis runs over, the one named last changes fastest.
Arguments:
- queries: bfloat16 [256, 32, 128], P(('parts', 'shard')), parts along dimension 0, may hold values from -6 to 6
- doc_tokens: bfloat16 [256, 128, 128], P(('parts', 'shard')), parts along dimension 0, may hold values from -0.5 to 0.5
- doc_lens: int32 [256], P(('parts', 'shard')), parts along dimension 0, may hold values from 1 to 128
- candidates: int32 [256, 128], P(('parts', 'shard')), parts along dimension 0, may hold values from 0 to 127
Outputs:
- scores: float32 [256, 128], P(('parts', 'shard')), parts along dimension 0
There are 2 independent parts, one for each index of `parts`. A program takes and returns all parts, laid end to end along the dimension named above; each array names one. Nothing has to cross between parts.
Inputs may be any that keep to these rules, and one draw needn't show every extreme that they name: `doc_lens`: every document has at least one live row. `candidates`: ids of documents of the same part.
All inputs are finite; a program needn't handle non-finite values.
Results may differ from a plain program's by a relative error of at most 0.0003.
Values may be sent and summed in bfloat16 or wider, within the bound.
A program may use at most 64 MiB of HBM per device.

v0:
```python
import jax
import jax.numpy as jnp
from jax import lax
from jax.sharding import PartitionSpec as P

QTOK = 32


def maxsim(query_rows, blocks, lengths):
    count, rows, width = blocks.shape
    tokens = query_rows.shape[0] // QTOK
    sim = lax.dot_general(
        query_rows,
        blocks.reshape(count * rows, width),
        (((1,), (1,)), ((), ())),
        preferred_element_type=jnp.float32,
    )
    sim = sim.reshape(tokens, QTOK, count, rows)
    live = jnp.arange(rows, dtype=jnp.int32)[None, :] < lengths[:, None]
    sim = jnp.where(live[None, None, :, :], sim, -1e30)
    return jnp.mean(jnp.max(sim, axis=3), axis=1)


def body(queries, doc_tokens, doc_lens, candidates):
    local_queries = queries.shape[0]
    local_docs = doc_tokens.shape[0]
    width = queries.shape[2]
    piece = lax.all_gather(queries, "shard", axis=0, tiled=True)
    count = piece.shape[0]
    groups = count // local_queries
    grouped = piece.reshape(groups, local_queries * QTOK, width)
    parts_out = lax.map(lambda rows_in: maxsim(rows_in, doc_tokens, doc_lens), grouped)
    owned = parts_out.reshape(count, local_docs)
    table = lax.all_to_all(owned, "shard", split_axis=0, concat_axis=1, tiled=True)
    return jnp.take_along_axis(table, candidates, axis=1)


def solution(mesh):
    in_specs = (
        P(("parts", "shard"), None, None),
        P(("parts", "shard"), None, None),
        P(("parts", "shard")),
        P(("parts", "shard"), None),
    )
    out_specs = P(("parts", "shard"), None)
    return jax.shard_map(body, mesh=mesh, in_specs=in_specs, out_specs=out_specs, check_vma=False)
```

profile of v0, /device:TPU:0, one launch (start us, length us, event | category | flops | bytes accessed | tf_op | source)
XLA Modules:
  0.0 122.0 jit_solution(7220427113552845102)
XLA Ops:
  7.3 42.8 %all-gather.2.cloned.1.call-done = bf16[128,32,128]{2,1,0:T(8,128)(2,1)} async-done(((bf16[8,32,128]{2,1,0:T(8,128)(2,1)}), bf16[128,32,128]{2,1,0:T(8,128)(2,1)}) %all-gather.2.cloned.1.call-update) | async-done | bytes 1048592 | tf_op jit(solution)/shard_map/all_gather | solution.py:28
  50.1 49.1 %while.10 = (s32[]{:T(128)}, f32[16,8,8]{2,1,0:T(8,128)}, s32[8]{0:T(128)S(1)}, bf16[16,256,128]{2,1,0:T(8,128)(2,1)}, bf16[8,128,128]{2,1,0:T(8,128)(2,1)}, /*index=5*/s32[]{:T(128)}, f32[]{:T(128)}) while((s32[]{:T(128)}, f32[16,8,8]{2,1,0:T(8,128)}, s32[8]{0:T(128)S(1)}, bf16[16,256,128]{2,1,0:T(8,128)(2,1)}, ...), condition=%wide.region_3.4_spmd, body=%wide.region_0.3_spmd.sunk | while | flops 67634176 | bytes 482421 | solution.py:32
  50.1 0.8 constant_dynamic-slice_fusion.2
  51.0 1.5 %fusion.9 = f32[8,32,8]{1,2,0:T(8,128)S(1)} fusion(bf16[8,32,128,1]{2,1,3,0:T(8,128)(2,1)S(1)} %bitcast.29, pred[8,128]{1,0:T(8,128)(4,1)S(1)} %iota_compare_fusion.2, bf16[8,128,128]{2,1,0:T(8,128)(2,1)} %get-tuple-element.92), kind=kOutput, calls=%fused_computation.2.clone.1 | convolution fusion | flops 67631104 | bytes 336896 | tf_op jit(solution)/shard_map/while/body/eval_jaxpr/dot_general | solution.py:12
  53.2 0.8 constant_dynamic-slice_fusion.2
  54.1 1.5 %fusion.9 = f32[8,32,8]{1,2,0:T(8,128)S(1)} fusion(bf16[8,32,128,1]{2,1,3,0:T(8,128)(2,1)S(1)} %bitcast.29, pred[8,128]{1,0:T(8,128)(4,1)S(1)} %iota_compare_fusion.2, bf16[8,128,128]{2,1,0:T(8,128)(2,1)} %get-tuple-element.92), kind=kOutput, calls=%fused_computation.2.clone.1 | convolution fusion | flops 67631104 | bytes 336896 | tf_op jit(solution)/shard_map/while/body/eval_jaxpr/dot_general | solution.py:12
  57.2 1.5 %fusion.9 = f32[8,32,8]{1,2,0:T(8,128)S(1)} fusion(bf16[8,32,128,1]{2,1,3,0:T(8,128)(2,1)S(1)} %bitcast.29, pred[8,128]{1,0:T(8,128)(4,1)S(1)} %iota_compare_fusion.2, bf16[8,128,128]{2,1,0:T(8,128)(2,1)} %get-tuple-element.92), kind=kOutput, calls=%fused_computation.2.clone.1 | convolution fusion | flops 67631104 | bytes 336896 | tf_op jit(solution)/shard_map/while/body/eval_jaxpr/dot_general | solution.py:12
  60.2 1.5 %fusion.9 = f32[8,32,8]{1,2,0:T(8,128)S(1)} fusion(bf16[8,32,128,1]{2,1,3,0:T(8,128)(2,1)S(1)} %bitcast.29, pred[8,128]{1,0:T(8,128)(4,1)S(1)} %iota_compare_fusion.2, bf16[8,128,128]{2,1,0:T(8,128)(2,1)} %get-tuple-element.92), kind=kOutput, calls=%fused_computation.2.clone.1 | convolution fusion | flops 67631104 | bytes 336896 | tf_op jit(solution)/shard_map/while/body/eval_jaxpr/dot_general | solution.py:12
  62.4 0.8 constant_dynamic-slice_fusion.2
  63.3 1.5 %fusion.9 = f32[8,32,8]{1,2,0:T(8,128)S(1)} fusion(bf16[8,32,128,1]{2,1,3,0:T(8,128)(2,1)S(1)} %bitcast.29, pred[8,128]{1,0:T(8,128)(4,1)S(1)} %iota_compare_fusion.2, bf16[8,128,128]{2,1,0:T(8,128)(2,1)} %get-tuple-element.92), kind=kOutput, calls=%fused_computation.2.clone.1 | convolution fusion | flops 67631104 | bytes 336896 | tf_op jit(solution)/shard_map/while/body/eval_jaxpr/dot_general | solution.py:12
  66.4 1.5 %fusion.9 = f32[8,32,8]{1,2,0:T(8,128)S(1)} fusion(bf16[8,32,128,1]{2,1,3,0:T(8,128)(2,1)S(1)} %bitcast.29, pred[8,128]{1,0:T(8,128)(4,1)S(1)} %iota_compare_fusion.2, bf16[8,128,128]{2,1,0:T(8,128)(2,1)} %get-tuple-element.92), kind=kOutput, calls=%fused_computation.2.clone.1 | convolution fusion | flops 67631104 | bytes 336896 | tf_op jit(solution)/shard_map/while/body/eval_jaxpr/dot_general | solution.py:12
  69.5 1.5 %fusion.9 = f32[8,32,8]{1,2,0:T(8,128)S(1)} fusion(bf16[8,32,128,1]{2,1,3,0:T(8,128)(2,1)S(1)} %bitcast.29, pred[8,128]{1,0:T(8,128)(4,1)S(1)} %iota_compare_fusion.2, bf16[8,128,128]{2,1,0:T(8,128)(2,1)} %get-tuple-element.92), kind=kOutput, calls=%fused_computation.2.clone.1 | convolution fusion | flops 67631104 | bytes 336896 | tf_op jit(solution)/shard_map/while/body/eval_jaxpr/dot_general | solution.py:12
  72.5 1.5 %fusion.9 = f32[8,32,8]{1,2,0:T(8,128)S(1)} fusion(bf16[8,32,128,1]{2,1,3,0:T(8,128)(2,1)S(1)} %bitcast.29, pred[8,128]{1,0:T(8,128)(4,1)S(1)} %iota_compare_fusion.2, bf16[8,128,128]{2,1,0:T(8,128)(2,1)} %get-tuple-element.92), kind=kOutput, calls=%fused_computation.2.clone.1 | convolution fusion | flops 67631104 | bytes 336896 | tf_op jit(solution)/shard_map/while/body/eval_jaxpr/dot_general | solution.py:12
  75.6 1.5 %fusion.9 = f32[8,32,8]{1,2,0:T(8,128)S(1)} fusion(bf16[8,32,128,1]{2,1,3,0:T(8,128)(2,1)S(1)} %bitcast.29, pred[8,128]{1,0:T(8,128)(4,1)S(1)} %iota_compare_fusion.2, bf16[8,128,128]{2,1,0:T(8,128)(2,1)} %get-tuple-element.92), kind=kOutput, calls=%fused_computation.2.clone.1 | convolution fusion | flops 67631104 | bytes 336896 | tf_op jit(solution)/shard_map/while/body/eval_jaxpr/dot_general | solution.py:12
  78.7 1.5 %fusion.9 = f32[8,32,8]{1,2,0:T(8,128)S(1)} fusion(bf16[8,32,128,1]{2,1,3,0:T(8,128)(2,1)S(1)} %bitcast.29, pred[8,128]{1,0:T(8,128)(4,1)S(1)} %iota_compare_fusion.2, bf16[8,128,128]{2,1,0:T(8,128)(2,1)} %get-tuple-element.92), kind=kOutput, calls=%fused_computation.2.clone.1 | convolution fusion | flops 67631104 | bytes 336896 | tf_op jit(solution)/shard_map/while/body/eval_jaxpr/dot_general | solution.py:12
  81.7 1.5 %fusion.9 = f32[8,32,8]{1,2,0:T(8,128)S(1)} fusion(bf16[8,32,128,1]{2,1,3,0:T(8,128)(2,1)S(1)} %bitcast.29, pred[8,128]{1,0:T(8,128)(4,1)S(1)} %iota_compare_fusion.2, bf16[8,128,128]{2,1,0:T(8,128)(2,1)} %get-tuple-element.92), kind=kOutput, calls=%fused_computation.2.clone.1 | convolution fusion | flops 67631104 | bytes 336896 | tf_op jit(solution)/shard_map/while/body/eval_jaxpr/dot_general | solution.py:12
  84.8 1.5 %fusion.9 = f32[8,32,8]{1,2,0:T(8,128)S(1)} fusion(bf16[8,32,128,1]{2,1,3,0:T(8,128)(2,1)S(1)} %bitcast.29, pred[8,128]{1,0:T(8,128)(4,1)S(1)} %iota_compare_fusion.2, bf16[8,128,128]{2,1,0:T(8,128)(2,1)} %get-tuple-element.92), kind=kOutput, calls=%fused_computation.2.clone.1 | convolution fusion | flops 67631104 | bytes 336896 | tf_op jit(solution)/shard_map/while/body/eval_jaxpr/dot_general | solution.py:12
  87.9 1.5 %fusion.9 = f32[8,32,8]{1,2,0:T(8,128)S(1)} fusion(bf16[8,32,128,1]{2,1,3,0:T(8,128)(2,1)S(1)} %bitcast.29, pred[8,128]{1,0:T(8,128)(4,1)S(1)} %iota_compare_fusion.2, bf16[8,128,128]{2,1,0:T(8,128)(2,1)} %get-tuple-element.92), kind=kOutput, calls=%fused_computation.2.clone.1 | convolution fusion | flops 67631104 | bytes 336896 | tf_op jit(solution)/shard_map/while/body/eval_jaxpr/dot_general | solution.py:12
  90.9 1.5 %fusion.9 = f32[8,32,8]{1,2,0:T(8,128)S(1)} fusion(bf16[8,32,128,1]{2,1,3,0:T(8,128)(2,1)S(1)} %bitcast.29, pred[8,128]{1,0:T(8,128)(4,1)S(1)} %iota_compare_fusion.2, bf16[8,128,128]{2,1,0:T(8,128)(2,1)} %get-tuple-element.92), kind=kOutput, calls=%fused_computation.2.clone.1 | convolution fusion | flops 67631104 | bytes 336896 | tf_op jit(solution)/shard_map/while/body/eval_jaxpr/dot_general | solution.py:12
  94.0 1.5 %fusion.9 = f32[8,32,8]{1,2,0:T(8,128)S(1)} fusion(bf16[8,32,128,1]{2,1,3,0:T(8,128)(2,1)S(1)} %bitcast.29, pred[8,128]{1,0:T(8,128)(4,1)S(1)} %iota_compare_fusion.2, bf16[8,128,128]{2,1,0:T(8,128)(2,1)} %get-tuple-element.92), kind=kOutput, calls=%fused_computation.2.clone.1 | convolution fusion | flops 67631104 | bytes 336896 | tf_op jit(solution)/shard_map/while/body/eval_jaxpr/dot_general | solution.py:12
  97.1 1.5 %fusion.9 = f32[8,32,8]{1,2,0:T(8,128)S(1)} fusion(bf16[8,32,128,1]{2,1,3,0:T(8,128)(2,1)S(1)} %bitcast.29, pred[8,128]{1,0:T(8,128)(4,1)S(1)} %iota_compare_fusion.2, bf16[8,128,128]{2,1,0:T(8,128)(2,1)} %get-tuple-element.92), kind=kOutput, calls=%fused_computation.2.clone.1 | convolution fusion | flops 67631104 | bytes 336896 | tf_op jit(solution)/shard_map/while/body/eval_jaxpr/dot_general | solution.py:12
  99.2 3.8 %all-to-all-start = ((f32[16,8,8]{2,1,0:T(8,128)}), f32[16,8,8]{2,1,0:T(8,128)S(1)}, u32[]{:S(2)}, u32[]{:S(2)}) async-start(f32[16,8,8]{2,1,0:T(8,128)} %get-tuple-element.32), calls=%async_computation | async-start | bytes 131072 | tf_op jit(solution)/shard_map/all_to_all | solution.py:34
  103.1 6.9 %all-to-all-done = f32[16,8,8]{2,1,0:T(8,128)S(1)} async-done(((f32[16,8,8]{2,1,0:T(8,128)}), f32[16,8,8]{2,1,0:T(8,128)S(1)}, u32[]{:S(2)}, u32[]{:S(2)}) %all-to-all-start) | async-done | bytes 4128 | tf_op jit(solution)/shard_map/all_to_all | solution.py:34
  110.1 4.5 %gather_fusion = f32[1024]{0:T(1024)S(1)} fusion(f32[8,128]{1,0:T(8,128)S(1)} %all_to_all.14, s32[1024]{0:T(1024)S(1)} %fusion.2), kind=kCustom, calls=%fused_computation | custom fusion | bytes 16384 | tf_op jit(solution)/shard_map/jit(take_along_axis)/gather | solution.py:35
  (72 shorter events, 24.5 us)
Async XLA Ops:
  6.5 43.6 %all-gather.2.cloned.1.call-start = ((), (), s32[]{:S(2)}) async-start(), calls=%async_computation.1 | async-start | bytes 1114112 | tf_op jit(solution)/shard_map/all_gather | solution.py:28
  7.3 42.9 %copy-start.1 = (s32[8]{0:T(128)S(1)}, s32[8]{0:T(128)}, u32[]{:S(2)}) copy-start(s32[8]{0:T(128)} %param.8) | copy-start | bytes 100
  99.2 3.8 %copy-start = (s32[8,128]{1,0:T(8,128)S(1)}, s32[8,128]{1,0:T(8,128)}, u32[]{:S(2)}) copy-start(s32[8,128]{1,0:T(8,128)} %param.9) | copy-start | bytes 12292
  99.2 10.7 %all-to-all-start = ((f32[16,8,8]{2,1,0:T(8,128)}), f32[16,8,8]{2,1,0:T(8,128)S(1)}, u32[]{:S(2)}, u32[]{:S(2)}) async-start(f32[16,8,8]{2,1,0:T(8,128)} %get-tuple-element.32), calls=%async_computation | async-start | bytes 131072 | tf_op jit(solution)/shard_map/all_to_all | solution.py:34
Sparse Core Ops, SparseCore 0:
  9.5 40.5 all-gather.1
where the time goes:
time: 123 us; the launch traced here: 122 us
  waiting for transfers between devices  50.4 us (41%)
  matrix products  23.4 us (19%)
  local copies, waits for them, and re-layouts  18.2 us (15%)
  between operations  13.4 us (11%)
  other arithmetic  12.7 us (10%)
  starting transfers between devices  3.81 us (3%)
    all_gather x1, waiting for transfers between devices, body(): piece = lax.all_gather(queries, 'shard', axis=0, tiled=True)  42.8 us
    dot_general x16, matrix products, maxsim(): lax.dot_general(query_rows, blocks.reshape(count * rows, width), (((1,),...  23.4 us
    dynamic_slice x16, local copies, waits for them, and re-layouts, body(): lax.map(lambda rows_in: maxsim(rows_in, doc_tokens, doc_lens), grouped)  13.5 us
    dynamic_update_slice x16, other arithmetic, body(): lax.map(lambda rows_in: maxsim(rows_in, doc_tokens, doc_lens), grouped)  9.6 us
    all_to_all x1, waiting for transfers between devices, body(): lax.all_to_all(owned, 'shard', split_axis=0, concat_axis=1, tiled=True)  6.87 us
    gather x1, local copies, waits for them, and re-layouts, body(): return jnp.take_along_axis(table, candidates, axis=1)  4.54 us
    all_to_all x1, starting transfers between devices, body(): lax.all_to_all(owned, 'shard', split_axis=0, concat_axis=1, tiled=True)  3.81 us
  transfers between devices with their start and end apart: 2, of which 2 were waited for; matrix products, arithmetic and copies ran while one was open for 0% of the time, Pallas kernels for 0%

commit v1 on v0

v1 whole, which is shorter than its diff:
```python
import functools

import jax
import jax.numpy as jnp
from jax import lax
from jax.experimental import pallas as pl
from jax.experimental.pallas import tpu as pltpu
from jax.sharding import PartitionSpec as P

LANES = 128
MESH = pl.DeviceIdType.MESH


def flip(index, mask):
    out = index
    bit = 1
    while bit <= mask:
        if mask & bit:
            out = out + bit - 2 * bit * ((index // bit) % 2)
        bit *= 2
    return out


def score_kernel(groups, chunks, tokens, lens_ref, q_hbm, d_hbm, table_ref,
                 qbuf, dbuf, best, outgoing, pieces,
                 local_sem, q_send, q_recv, p_send, p_recv, y_send, y_recv, r_send, r_recv, o_send, o_recv):
    part = lax.axis_index("parts")
    me = lax.axis_index("shard")
    k = lax.rem(me, 2)
    b = lax.rem(me // 2, 2)
    g = me // 4

    def at(g_, b_, k_):
        return (part, g_ * 4 + b_ * 2 + k_)

    docs, rows, width = d_hbm.shape
    q_rows = q_hbm.shape[0]
    count = q_rows // tokens
    per_group = 4 * docs
    slot_me = b * 2 + k
    slot_partner = b * 2 + 1 - k
    slot_y = (1 - b) * 2 + k
    slot_yp = (1 - b) * 2 + 1 - k
    step = docs // chunks

    peers = [at(flip(g, j), b, k) for j in range(1, groups)]
    partner = at(g, b, 1 - k)
    across = at(g, 1 - b, k)

    q_in = pltpu.make_async_copy(q_hbm, qbuf.at[g], local_sem.at[0])
    d_in = pltpu.make_async_copy(d_hbm, dbuf.at[slot_me], local_sem.at[1])
    q_in.start()
    d_in.start()

    barrier = pltpu.get_barrier_semaphore()
    for peer in peers + [partner, across]:
        pl.semaphore_signal(barrier, inc=1, device_id=peer, device_id_type=MESH)

    best[...] = jnp.zeros_like(best)
    d_in.wait()
    row_of = lax.broadcasted_iota(jnp.int32, (rows, width), 0)
    for j in range(docs):
        block = dbuf[slot_me, j]
        first = jnp.broadcast_to(block[0:1, :].astype(jnp.float32), (rows, width))
        kept = jnp.where(row_of < lens_ref[j], block.astype(jnp.float32), first)
        dbuf[slot_me, j] = kept.astype(dbuf.dtype)
    q_in.wait()
    pl.semaphore_wait(barrier, len(peers) + 2)

    def remote(src, dst, send, recv, device):
        return pltpu.make_async_remote_copy(src_ref=src, dst_ref=dst, send_sem=send, recv_sem=recv,
                                            device_id=device, device_id_type=MESH)

    def send_queries(j):
        return remote(qbuf.at[g], qbuf.at[g], q_send.at[j - 1], q_recv.at[j - 1], peers[j - 1])

    def doc_chunk(slot, c, send, recv, device):
        ref = dbuf.at[slot, pl.ds(c * step, step)]
        return remote(ref, ref, send.at[c], recv.at[c], device)

    to_partner = remote(dbuf.at[slot_me], dbuf.at[slot_me], p_send, p_recv, partner)
    to_across = [doc_chunk(slot_me, c, y_send, y_recv, across) for c in range(chunks)]
    relays = [doc_chunk(slot_y, c, r_send, r_recv, partner) for c in range(chunks)]
    q_out = [send_queries(j) for j in range(1, groups)]

    to_partner.start()
    if q_out:
        q_out[0].start()
    to_across[0].start()
    for copy in q_out[1:]:
        copy.start()
    for copy in to_across[1:]:
        copy.start()

    base = lax.rem(g, LANES // per_group) * per_group

    def score(j, slot):
        owner = flip(g, j)
        block = dbuf[slot].reshape(docs * rows, width)
        sim = lax.dot_general(block, qbuf[owner], (((1,), (1,)), ((), ())),
                              preferred_element_type=jnp.float32)
        top = jnp.max(sim.reshape(docs, rows, q_rows), axis=1)
        best[j, pl.ds(pl.multiple_of(base + slot * docs, docs), docs), :] = top

    q_of = lax.broadcasted_iota(jnp.int32, (count, q_rows), 1) // tokens
    pick = (q_of == lax.broadcasted_iota(jnp.int32, (count, q_rows), 0)).astype(jnp.float32)
    pick = (pick * (1.0 / tokens)).astype(jnp.bfloat16)

    def reduce_tokens(j):
        rest = best[j]
        total = jnp.zeros((count, LANES), jnp.float32)
        for _ in range(3):
            term = rest.astype(jnp.bfloat16)
            rest = rest - term.astype(jnp.float32)
            total += lax.dot_general(pick, term, (((1,), (1,)), ((), ())),
                                     preferred_element_type=jnp.float32)
        return total

    results = []

    def give(j):
        outgoing[j] = reduce_tokens(j)
        copy = remote(outgoing.at[j], pieces.at[g], o_send.at[j - 1], o_recv.at[j - 1], peers[j - 1])
        copy.start()
        results.append(copy)

    def wait_queries(j):
        q_out[j - 1].wait_recv()

    def pass_on(c):
        to_across[c].wait_recv()
        relays[c].start()

    score(0, slot_me)
    to_partner.wait_recv()
    score(0, slot_partner)
    passed = 0
    last = groups - 1
    for j in range(1, last):
        if passed < chunks:
            pass_on(passed)
            passed += 1
        wait_queries(j)
        score(j, slot_me)
        score(j, slot_partner)
    while passed < chunks:
        pass_on(passed)
        passed += 1
    for j in range(last):
        score(j, slot_y)
    for c in range(chunks):
        relays[c].wait_recv()
    for j in range(1, last):
        score(j, slot_yp)
        give(j)
    wait_queries(last)
    for slot in (slot_me, slot_partner, slot_y, slot_yp):
        score(last, slot)
    give(last)
    score(0, slot_yp)
    pieces[g] = reduce_tokens(0)

    for copy in [to_partner] + to_across + relays + q_out:
        copy.wait_send()
    for copy in results:
        copy.wait_recv()
    wide = LANES // per_group
    for n in range(table_ref.shape[1] // LANES):
        total = pieces[n * wide]
        for s in range(n * wide + 1, (n + 1) * wide):
            total += pieces[s]
        table_ref[:, n * LANES:(n + 1) * LANES] = total
    for copy in results:
        copy.wait_send()


def gather_kernel(table_ref, cand_ref, out_ref):
    cand = cand_ref[...]
    inside = lax.rem(cand, LANES)
    which = cand // LANES
    out = None
    for n in range(table_ref.shape[1] // LANES):
        got = jnp.take_along_axis(table_ref[:, n * LANES:(n + 1) * LANES], inside, axis=1,
                                  mode="promise_in_bounds")
        out = got if out is None else jnp.where(which == n, got, out)
    out_ref[...] = out


def body(shards, queries, doc_tokens, doc_lens, candidates):
    count, tokens, width = queries.shape
    docs, rows, _ = doc_tokens.shape
    groups = shards // 4
    chunks = 4
    q_rows = count * tokens
    dma = pltpu.SemaphoreType.DMA
    others = groups - 1
    table = pl.pallas_call(
        functools.partial(score_kernel, groups, chunks, tokens),
        out_shape=jax.ShapeDtypeStruct((count, shards * docs), jnp.float32),
        in_specs=[
            pl.BlockSpec(memory_space=pltpu.SMEM),
            pl.BlockSpec(memory_space=pl.ANY),
            pl.BlockSpec(memory_space=pl.ANY),
        ],
        out_specs=pl.BlockSpec(memory_space=pltpu.VMEM),
        scratch_shapes=[
            pltpu.VMEM((groups, q_rows, width), queries.dtype),
            pltpu.VMEM((4, docs, rows, width), doc_tokens.dtype),
            pltpu.VMEM((groups, LANES, q_rows), jnp.float32),
            pltpu.VMEM((groups, count, LANES), jnp.float32),
            pltpu.VMEM((groups, count, LANES), jnp.float32),
            dma((2,)),
            dma((others,)), dma((others,)),
            dma, dma,
            dma((chunks,)), dma((chunks,)),
            dma((chunks,)), dma((chunks,)),
            dma((others,)), dma((others,)),
        ],
        compiler_params=pltpu.CompilerParams(collective_id=0, has_side_effects=True),
    )(doc_lens, queries.reshape(q_rows, width), doc_tokens)
    return pl.pallas_call(
        gather_kernel,
        out_shape=jax.ShapeDtypeStruct(candidates.shape, jnp.float32),
    )(table, candidates)


def solution(mesh):
    in_specs = (
        P(("parts", "shard"), None, None),
        P(("parts", "shard"), None, None),
        P(("parts", "shard")),
        P(("parts", "shard"), None),
    )
    out_specs = P(("parts", "shard"), None)
    step = functools.partial(body, mesh.shape["shard"])
    return jax.shard_map(step, mesh=mesh, in_specs=in_specs, out_specs=out_specs, check_vma=False)
```

time: 123 us -> 21.6 us (0.18)
  waiting for transfers between devices: 50.4 us -> 0 us
  matrix products: 23.4 us -> 0 us
  Pallas kernels: 0 us -> 21.4 us
  local copies, waits for them, and re-layouts: 18.2 us -> 0 us
  between operations: 13.4 us -> 0.01 us
  other arithmetic: 12.7 us -> 0 us
  starting transfers between devices: 3.81 us -> 0 us
    all_gather x1 -> x0, waiting for transfers between devices: 42.8 us -> none  [body(): piece = lax.all_gather(queries, 'shard', axis=0, tiled=True)]
    dot_general x16 -> x0, matrix products: 23.4 us -> none  [maxsim(): lax.dot_general(query_rows, blocks.reshape(count * rows, width), (((1,),...]
    pallas_call x0 -> x2, Pallas kernels: none -> 21.4 us  [the longest x1 20.1 us: body(): pl.pallas_call(functools.partial(score_kernel, groups, chunks, tokens), o...]
    dynamic_slice x16 -> x0, local copies, waits for them, and re-layouts: 13.5 us -> none  [body(): lax.map(lambda rows_in: maxsim(rows_in, doc_tokens, doc_lens), grouped)]
    dynamic_update_slice x16 -> x0, other arithmetic: 9.6 us -> none  [body(): lax.map(lambda rows_in: maxsim(rows_in, doc_tokens, doc_lens), grouped)]
    all_to_all x1 -> x0, waiting for transfers between devices: 6.87 us -> none  [body(): lax.all_to_all(owned, 'shard', split_axis=0, concat_axis=1, tiled=True)]
    gather x1 -> x0, local copies, waits for them, and re-layouts: 4.54 us -> none  [body(): return jnp.take_along_axis(table, candidates, axis=1)]
    all_to_all x1 -> x0, starting transfers between devices: 3.81 us -> none  [body(): lax.all_to_all(owned, 'shard', split_axis=0, concat_axis=1, tiled=True)]
  transfers between devices with their start and end apart: 2 -> 0, of which waited for: 2 -> 0; matrix products, arithmetic and copies ran while one was open for 0% -> 0% of each run, Pallas kernels for 0% -> 0%
where the time goes in v1:
time: 21.6 us; the launch traced here: 21.4 us
  Pallas kernels  21.4 us (99%)
    pallas_call x1, Pallas kernels, body(): pl.pallas_call(functools.partial(score_kernel, groups, chunks, tokens), o...  20.1 us
    pallas_call x1, Pallas kernels, body(): pl.pallas_call(gather_kernel, out_shape=jax.ShapeDtypeStruct(candidates.s...  1.36 us

profile of v1, /device:TPU:0, one launch (start us, length us, event | category | flops | bytes accessed | tf_op | source)
XLA Modules:
  0.0 21.4 jit_solution(13113619447616924912)
XLA Ops:
  0.0 20.1 %shard_map.46.table_ref = f32[8,128]{1,0:T(8,128)} custom-call(s32[8]{0:T(128)} %lens_ref.1, bf16[256,128]{1,0:T(8,128)(2,1)} %bitcast.1, bf16[8,128,128]{2,1,0:T(8,128)(2,1)} %d_hbm.1), custom_call_target="tpu_custom_call" | custom-call | tf_op jit(solution)/shard_map/pallas_call | solution.py:197
  20.1 1.4 %shard_map.47 = f32[8,128]{1,0:T(8,128)} custom-call(f32[8,128]{1,0:T(8,128)} %shard_map.46.table_ref, s32[8,128]{1,0:T(8,128)} %cand_ref.1), custom_call_target="tpu_custom_call" | custom-call | tf_op jit(solution)/shard_map/pallas_call | solution.py:221

commit v2 on v1

v2 whole, which is shorter than its diff:
```python
import functools

import jax
import jax.numpy as jnp
from jax import lax
from jax.experimental import pallas as pl
from jax.experimental.pallas import tpu as pltpu
from jax.sharding import PartitionSpec as P

LANES = 128
MESH = pl.DeviceIdType.MESH


def flip(index, mask):
    out = index
    bit = 1
    while bit <= mask:
        if mask & bit:
            out = out + bit - 2 * bit * ((index // bit) % 2)
        bit *= 2
    return out


def score_kernel(groups, chunks, tokens, lens_ref, q_hbm, d_hbm, table_ref,
                 qbuf, dbuf, best, outgoing, pieces,
                 local_sem, q_send, q_recv, p_send, p_recv, y_send, y_recv, f_send, f_recv, o_send, o_recv):
    part = lax.axis_index("parts")
    me = lax.axis_index("shard")
    k = lax.rem(me, 2)
    b = lax.rem(me // 2, 2)
    g = me // 4

    def at(g_, b_, k_):
        return (part, g_ * 4 + b_ * 2 + k_)

    docs, rows, width = d_hbm.shape
    q_rows = q_hbm.shape[0]
    count = q_rows // tokens
    step = docs // chunks
    slots = {name: b_ * 2 + k_ for name, b_, k_ in
             (("me", b, k), ("partner", b, 1 - k), ("y", 1 - b, k), ("yp", 1 - b, 1 - k))}
    partner = at(g, b, 1 - k)
    across = at(g, 1 - b, k)
    order = [1] + [j for j in range(groups - 1, 1, -1)]

    q_in = pltpu.make_async_copy(q_hbm, qbuf.at[g], local_sem.at[0])
    d_in = pltpu.make_async_copy(d_hbm, dbuf.at[slots["me"]], local_sem.at[1])
    d_in.start()
    q_in.start()

    barrier = pltpu.get_barrier_semaphore()
    takers = [at(flip(g, j), b, k) for j in order]
    for peer in takers + [partner, across]:
        pl.semaphore_signal(barrier, inc=1, device_id=peer, device_id_type=MESH)

    d_in.wait()
    row_of = lax.broadcasted_iota(jnp.int32, (rows, width), 0)
    for j in range(docs):
        block = dbuf[slots["me"], j]
        first = jnp.broadcast_to(block[0:1, :].astype(jnp.float32), (rows, width))
        kept = jnp.where(row_of < lens_ref[j], block.astype(jnp.float32), first)
        dbuf[slots["me"], j] = kept.astype(dbuf.dtype)
    q_in.wait()
    pl.semaphore_wait(barrier, len(takers) + 2)

    def remote(src, dst, send, recv, device):
        return pltpu.make_async_remote_copy(src_ref=src, dst_ref=dst, send_sem=send, recv_sem=recv,
                                            device_id=device, device_id_type=MESH)

    def doc_chunk(name, c, send, recv, device):
        ref = dbuf.at[slots[name], pl.ds(c * step, step)]
        return remote(ref, ref, send.at[c], recv.at[c], device)

    mine = dbuf.at[slots["me"]]
    to_partner = remote(mine, mine, p_send, p_recv, partner)
    to_across = [doc_chunk("me", c, y_send, y_recv, across) for c in range(chunks)]
    relays = [doc_chunk("y", c, f_send, f_recv, partner) for c in range(chunks)]
    q_out = {j: remote(qbuf.at[g], qbuf.at[g], q_send.at[j], q_recv.at[j], peer) for j, peer in zip(order, takers)}

    to_across[0].start()
    for j in order[:2]:
        q_out[j].start()
    to_partner.start()
    for j in order[2:]:
        q_out[j].start()
    for copy in to_across[1:]:
        copy.start()

    have = {name: 0 for name in slots}
    done = {}
    ready = []

    def dot_max(j, name, low, high):
        n = high - low
        u = flip(g, j)
        block = dbuf[slots[name], low:high].reshape(n * rows, width)
        sim = lax.dot_general(block, qbuf[u], (((1,), (1,)), ((), ())), preferred_element_type=jnp.float32)
        best[u * 4 + slots[name], low:high, :] = jnp.max(sim.reshape(n, rows, q_rows), axis=1)

    def catch_up():
        for name in slots:
            for j in ready:
                low = done.get((j, name), 0)
                if low < have[name]:
                    dot_max(j, name, low, have[name])
                    done[j, name] = have[name]

    def arrive(event):
        kind, which = event
        if kind == "q":
            q_out[which].wait_recv()
            ready.append(which)
        elif kind == "p":
            to_partner.wait_recv()
            have["partner"] = docs
        elif kind == "y":
            to_across[which].wait_recv()
            relays[which].start()
            have["y"] += step
        else:
            relays[which].wait_recv()
            have["yp"] += step

    ready.append(0)
    have["me"] = docs
    catch_up()
    arrive(("p", 0))
    catch_up()
    queue = [("q", j) for j in order]
    events = []
    for c in range(chunks):
        if queue:
            events.append(queue.pop(0))
        events.append(("y", c))
        if c > 0:
            events.append(("yp", c - 1))
    for event in queue:
        events.insert(len(events) - 2, event)
    events.append(("yp", chunks - 1))
    for event in events:
        arrive(event)
        catch_up()

    q_of = lax.broadcasted_iota(jnp.int32, (count, q_rows), 1) // tokens
    pick = (q_of == lax.broadcasted_iota(jnp.int32, (count, q_rows), 0)).astype(jnp.float32)
    pick = (pick * (1.0 / tokens)).astype(jnp.bfloat16)
    rest = best[...].reshape(groups * 4 * docs, q_rows)
    total = None
    for _ in range(3):
        term = rest.astype(jnp.bfloat16)
        rest = rest - term.astype(jnp.float32)
        got = lax.dot_general(pick, term, (((1,), (1,)), ((), ())), preferred_element_type=jnp.float32)
        total = got if total is None else total + got
    blocks = total.shape[1] // LANES
    for n in range(blocks):
        outgoing[n] = total[:, n * LANES:(n + 1) * LANES]

    results = [remote(outgoing, pieces.at[g], o_send.at[i], o_recv.at[i], peer) for i, peer in enumerate(takers)]
    for copy in results[::-1]:
        copy.start()
    pieces[g] = outgoing[...]
    for copy in to_across + relays + [to_partner] + list(q_out.values()):
        copy.wait_send()

    per_unit = 4 * docs
    inside = LANES // per_unit
    lane = lax.broadcasted_iota(jnp.int32, (count, LANES), 1) // per_unit
    for copy in results:
        copy.wait_recv()
    for n in range(table_ref.shape[1] // LANES):
        total = None
        for i in range(inside):
            shift = lax.rem(i - lax.rem(g, inside) + inside, inside) * per_unit
            got = pltpu.roll(pieces[n * inside + i, g // inside], shift, 1)
            total = got if total is None else jnp.where(lane == i, got, total)
        table_ref[:, n * LANES:(n + 1) * LANES] = total
    for copy in results:
        copy.wait_send()


def gather_kernel(table_ref, cand_ref, out_ref):
    cand = cand_ref[...]
    inside = lax.rem(cand, LANES)
    which = cand // LANES
    out = None
    for n in range(table_ref.shape[1] // LANES):
        got = jnp.take_along_axis(table_ref[:, n * LANES:(n + 1) * LANES], inside, axis=1,
                                  mode="promise_in_bounds")
        out = got if out is None else jnp.where(which == n, got, out)
    out_ref[...] = out


def body(shards, queries, doc_tokens, doc_lens, candidates):
    count, tokens, width = queries.shape
    docs, rows, _ = doc_tokens.shape
    groups = shards // 4
    chunks = 2
    q_rows = count * tokens
    blocks = groups * 4 * docs // LANES
    dma = pltpu.SemaphoreType.DMA
    table = pl.pallas_call(
        functools.partial(score_kernel, groups, chunks, tokens),
        out_shape=jax.ShapeDtypeStruct((count, shards * docs), jnp.float32),
        in_specs=[
            pl.BlockSpec(memory_space=pltpu.SMEM),
            pl.BlockSpec(memory_space=pl.ANY),
            pl.BlockSpec(memory_space=pl.ANY),
        ],
        out_specs=pl.BlockSpec(memory_space=pltpu.VMEM),
        scratch_shapes=[
            pltpu.VMEM((groups, q_rows, width), queries.dtype),
            pltpu.VMEM((4, docs, rows, width), doc_tokens.dtype),
            pltpu.VMEM((groups * 4, docs, q_rows), jnp.float32),
            pltpu.VMEM((blocks, count, LANES), jnp.float32),
            pltpu.VMEM((groups, blocks, count, LANES), jnp.float32),
            dma((2,)),
            dma((groups,)), dma((groups,)),
            dma, dma,
            dma((chunks,)), dma((chunks,)),
            dma((chunks,)), dma((chunks,)),
            dma((groups,)), dma((groups,)),
        ],
        compiler_params=pltpu.CompilerParams(collective_id=0, has_side_effects=True),
    )(doc_lens, queries.reshape(q_rows, width), doc_tokens)
    return pl.pallas_call(
        gather_kernel,
        out_shape=jax.ShapeDtypeStruct(candidates.shape, jnp.float32),
    )(table, candidates)


def solution(mesh):
    in_specs = (
        P(("parts", "shard"), None, None),
        P(("parts", "shard"), None, None),
        P(("parts", "shard")),
        P(("parts", "shard"), None),
    )
    out_specs = P(("parts", "shard"), None)
    step = functools.partial(body, mesh.shape["shard"])
    return jax.shard_map(step, mesh=mesh, in_specs=in_specs, out_specs=out_specs, check_vma=False)
```

time: 21.6 us -> 21 us (0.972)
  Pallas kernels: 21.4 us -> 20.8 us
    pallas_call x1, Pallas kernels: 20.1 us -> 19.4 us  [body(): pl.pallas_call(functools.partial(score_kernel, groups, chunks, tokens), o...]
where the time goes in v2:
time: 21 us; the launch traced here: 20.8 us
  Pallas kernels  20.8 us (99%)
    pallas_call x1, Pallas kernels, body(): pl.pallas_call(functools.partial(score_kernel, groups, chunks, tokens), o...  19.4 us
    pallas_call x1, Pallas kernels, body(): pl.pallas_call(gather_kernel, out_shape=jax.ShapeDtypeStruct(candidates.s...  1.36 us

profile of v2, /device:TPU:0, one launch (start us, length us, event | category | flops | bytes accessed | tf_op | source)
XLA Modules:
  0.0 20.8 jit_solution(2594151634443804314)
XLA Ops:
  0.0 19.4 %shard_map.46.table_ref = f32[8,128]{1,0:T(8,128)} custom-call(s32[8]{0:T(128)} %lens_ref.1, bf16[256,128]{1,0:T(8,128)(2,1)} %bitcast.1, bf16[8,128,128]{2,1,0:T(8,128)(2,1)} %d_hbm.1), custom_call_target="tpu_custom_call" | custom-call | tf_op jit(solution)/shard_map/pallas_call | solution.py:201
  19.4 1.4 %shard_map.47 = f32[8,128]{1,0:T(8,128)} custom-call(f32[8,128]{1,0:T(8,128)} %shard_map.46.table_ref, s32[8,128]{1,0:T(8,128)} %cand_ref.1), custom_call_target="tpu_custom_call" | custom-call | tf_op jit(solution)/shard_map/pallas_call | solution.py:225
